TPU v7x, 32 devices: a whole 2x2x4 slice. The times are simulated.
32 devices in a mesh: grp: 2 (over x), row: 8 (over z, core), col: 2 (over y).
Axes of the slice: x: 2, y: 2, z: 4, core: 2. Of those that a mesh axis runs over, the one named last changes fastest.
Arguments:
- vectors: float32 [64, 128, 512], P('grp', 'row', 'col'), may hold values from -6 to 6
- disorder: float32 [128, 512], P('row', 'col'), may hold values from -1.5 to 1.5
Outputs:
- cheb_prev: float32 [64, 128, 512], P('grp', 'row', 'col')
- cheb_last: float32 [64, 128, 512], P('grp', 'row', 'col')
- moments: float32 [17], replicated
All inputs are finite; a program needn't handle non-finite values.
Results may differ from a plain program's by a relative error of at most 0.0001.
Values sent between devices are 32-bit elements; how exact they have to be, the bound alone decides.
No kernel may reach another device: no remote copies, remote signals or barrier semaphores. Data moves between devices by JAX's collectives and lax.ppermute only.
A program may use at most 64 MiB of HBM per device.

v0:
```python
import jax
import jax.numpy as jnp
from jax import lax
from jax.sharding import PartitionSpec as P

STEPS = 8
SCALE = 4.6


def extended(block, sides, width):
    for axis, dim in sides:
        count = lax.axis_size(axis)
        forward = [(i, i + 1) for i in range(count - 1)]
        forward.append((count - 1, 0))
        backward = [(target, source) for source, target in forward]
        low = lax.ppermute(
            lax.slice_in_dim(block, block.shape[dim] - width, None, axis=dim), axis, forward
        )
        high = lax.ppermute(lax.slice_in_dim(block, 0, width, axis=dim), axis, backward)
        block = jnp.concatenate([low, block, high], axis=dim)
    return block


def inner_hop(field, dis_part, even_part):
    left = field[:, 1:-1, :-2]
    right = field[:, 1:-1, 2:]
    below = field[:, 2:, 1:-1]
    above = field[:, :-2, 1:-1]
    center = field[:, 1:-1, 1:-1]
    vertical = jnp.where(even_part, below, above)
    return (dis_part * center - (left + right + vertical)) / SCALE


def body(vectors, disorder):
    vecs, rows_here, cols_here = vectors.shape
    count = float(
        vecs
        * lax.axis_size("grp")
        * rows_here
        * lax.axis_size("row")
        * cols_here
        * lax.axis_size("col")
    )
    margin = 4
    dis_pad = extended(disorder, (("row", 0), ("col", 1)), margin)
    rows = lax.broadcasted_iota(jnp.int32, dis_pad.shape, 0)
    cols = lax.broadcasted_iota(jnp.int32, dis_pad.shape, 1)
    even_pad = (rows + cols) % 2 == 0

    def advance(field):
        extra = (field.shape[1] - rows_here) // 2
        start = margin - extra
        stop_r = start + field.shape[1] - 1
        stop_c = start + field.shape[2] - 1
        dis_part = dis_pad[start + 1 : stop_r, start + 1 : stop_c]
        even_part = even_pad[start + 1 : stop_r, start + 1 : stop_c][None]
        return inner_hop(field, dis_part, even_part)

    def interior(field):
        extra = (field.shape[1] - rows_here) // 2
        return field[:, extra : extra + rows_here, extra : extra + cols_here]

    older = vectors
    newer = vectors
    squares = [jnp.sum(vectors * vectors)]
    crosses = []
    for rounds in range(STEPS // margin):
        padded_old, padded_new = (
            extended(older, (("row", 1), ("col", 2)), margin),
            extended(newer, (("row", 1), ("col", 2)), margin),
        )
        for inner in range(margin):
            if rounds == 0 and inner == 0:
                latest = advance(padded_new)
            else:
                latest = 2.0 * advance(padded_new) - padded_old[:, 1:-1, 1:-1]
            padded_old = padded_new[:, 1:-1, 1:-1]
            padded_new = latest
            kept_new = interior(padded_new)
            kept_old = interior(padded_old)
            squares.append(jnp.sum(kept_new * kept_new))
            crosses.append(jnp.sum(kept_new * kept_old))
        older, newer = (padded_old, padded_new)
    total_squares = [lax.psum(squares[0], ("grp", "row", "col"))]
    total_crosses = []
    for index in range(STEPS):
        pair = lax.psum((squares[index + 1], crosses[index]), ("grp", "row", "col"))
        total_squares.append(pair[0])
        total_crosses.append(pair[1])
    total_squares = jnp.stack(total_squares)
    total_crosses = jnp.stack(total_crosses)
    total_squares = total_squares / count
    total_crosses = total_crosses / count
    first = total_squares[0]
    second = total_crosses[0]
    values = [first, second]
    for index in range(1, STEPS + 1):
        values.append(2.0 * total_squares[index] - first)
        if index < STEPS:
            values.append(2.0 * total_crosses[index] - second)
    return (older, newer, jnp.stack(values))


def solution(mesh):
    placed = (P("grp", "row", "col"), P("row", "col"))
    return jax.shard_map(
        body,
        mesh=mesh,
        in_specs=placed,
        out_specs=(P("grp", "row", "col"), P("grp", "row", "col"), P()),
        check_vma=False,
    )
```

profile of v0, /device:TPU:0, one launch (start us, length us, event | category | flops | bytes accessed | tf_op | source)
XLA Modules:
  0.0 162.1 jit_solution(18027950216888657291)
XLA Ops:
  1.8 4.0 %collective-permute-start.1 = (f32[4,256]{1,0:T(4,128)S(1)}, f32[4,256]{1,0:T(4,128)S(1)}, u32[]{:S(2)}, u32[]{:S(2)}) collective-permute-start(f32[4,256]{1,0:T(4,128)S(1)} %get-tuple-element.64), channel_id=1, source_target_pairs={{2,0},{4,2},{6,4},{8,6},{10,8},{12,10},{14,12},{0,14},{3,1},{5,3},... | collective-permute-start | bytes 12296 | tf_op jit(solution)/shard_map/ppermute | solution.py:19
  5.9 1.1 fusion.39
  7.0 3.5 %collective-permute-start.5 = (f32[32,4,256]{2,1,0:T(4,128)S(1)}, f32[32,4,256]{2,1,0:T(4,128)S(1)}, u32[]{:S(2)}, u32[]{:S(2)}) collective-permute-start(f32[32,4,256]{2,1,0:T(4,128)S(1)} %get-tuple-element.60), channel_id=1, source_target_pairs={{2,0},{4,2},{6,4},{8,6},{10,8},{12,10},{14,12},{0,14},{3,1},{5,3},... | collective-permute-start | bytes 393224 | tf_op jit(solution)/shard_map/ppermute | solution.py:19
  10.9 0.7 pad_maximum_fusion.10
  11.7 2.0 %collective-permute-start.2 = (f32[24,4]{1,0:T(8,128)S(1)}, f32[24,4]{1,0:T(8,128)S(1)}, u32[]{:S(2)}, u32[]{:S(2)}) collective-permute-start(f32[24,4]{1,0:T(8,128)S(1)} %get-tuple-element.61), channel_id=1, source_target_pairs={{0,1},{1,0},{2,3},{3,2},{4,5},{5,4},{6,7},{7,6},{8,9},{9,8},{10,11... | collective-permute-start | bytes 1160 | tf_op jit(solution)/shard_map/ppermute | solution.py:16
  13.8 1.2 pad_maximum_fusion.6
  15.2 2.6 %collective-permute-start.6 = (f32[32,24,4]{2,1,0:T(8,128)S(1)}, f32[32,24,4]{2,1,0:T(8,128)S(1)}, u32[]{:S(2)}, u32[]{:S(2)}) collective-permute-start(f32[32,24,4]{2,1,0:T(8,128)S(1)} %get-tuple-element.55), channel_id=1, source_target_pairs={{0,1},{1,0},{2,3},{3,2},{4,5},{5,4},{6,7},{7,6},{8,9},{9,8},{10,11... | collective-permute-start | bytes 36872 | tf_op jit(solution)/shard_map/ppermute | solution.py:16
  18.2 9.5 %collective-permute-done.6 = f32[32,24,4]{2,1,0:T(8,128)S(1)} collective-permute-done((f32[32,24,4]{2,1,0:T(8,128)S(1)}, f32[32,24,4]{2,1,0:T(8,128)S(1)}, u32[]{:S(2)}, u32[]{:S(2)}) %collective-permute-start.6) | collective-permute-done | bytes 12320 | tf_op jit(solution)/shard_map/ppermute | solution.py:16
  27.7 6.4 %collective-permute-done.7 = f32[32,24,4]{2,1,0:T(8,128)S(1)} collective-permute-done((f32[32,24,4]{2,1,0:T(8,128)S(1)}, f32[32,24,4]{2,1,0:T(8,128)S(1)}, u32[]{:S(2)}, u32[]{:S(2)}) %collective-permute-start.7) | collective-permute-done | bytes 12320 | tf_op jit(solution)/shard_map/ppermute | solution.py:19
  34.8 1.3 fusion.18
  36.1 1.6 slice_subtract_fusion.3
  37.7 1.6 slice_subtract_fusion.2
  39.3 0.7 fusion.34
  40.2 3.5 %collective-permute-start.9 = (f32[32,4,256]{2,1,0:T(4,128)S(1)}, f32[32,4,256]{2,1,0:T(4,128)S(1)}, u32[]{:S(2)}, u32[]{:S(2)}) collective-permute-start(f32[32,4,256]{2,1,0:T(4,128)S(1)} %get-tuple-element.58), channel_id=1, source_target_pairs={{2,0},{4,2},{6,4},{8,6},{10,8},{12,10},{14,12},{0,14},{3,1},{5,3},... | collective-permute-start | bytes 393224 | tf_op jit(solution)/shard_map/ppermute | solution.py:19
  44.0 3.5 %collective-permute-start.13 = (f32[32,4,256]{2,1,0:T(4,128)S(1)}, f32[32,4,256]{2,1,0:T(4,128)S(1)}, u32[]{:S(2)}, u32[]{:S(2)}) collective-permute-start(f32[32,4,256]{2,1,0:T(4,128)S(1)} %get-tuple-element.48), channel_id=1, source_target_pairs={{2,0},{4,2},{6,4},{8,6},{10,8},{12,10},{14,12},{0,14},{3,1},{5,3},... | collective-permute-start | bytes 393224 | tf_op jit(solution)/shard_map/ppermute | solution.py:19
  48.4 1.8 %collective-permute-start.11 = (f32[32,24,4]{2,1,0:T(8,128)S(1)}, f32[32,24,4]{2,1,0:T(8,128)S(1)}, u32[]{:S(2)}, u32[]{:S(2)}) collective-permute-start(f32[32,24,4]{2,1,0:T(8,128)S(1)} %get-tuple-element.54), channel_id=1, source_target_pairs={{1,0},{0,1},{3,2},{2,3},{5,4},{4,5},{7,6},{6,7},{9,8},{8,9},{11,10... | collective-permute-start | bytes 36872 | tf_op jit(solution)/shard_map/ppermute | solution.py:19
  50.6 0.8 collective-permute-start.14
  51.3 1.3 collective-permute-start.15
  52.7 7.5 %collective-permute-done.10 = f32[32,24,4]{2,1,0:T(8,128)S(1)} collective-permute-done((f32[32,24,4]{2,1,0:T(8,128)S(1)}, f32[32,24,4]{2,1,0:T(8,128)S(1)}, u32[]{:S(2)}, u32[]{:S(2)}) %collective-permute-start.10) | collective-permute-done | bytes 12320 | tf_op jit(solution)/shard_map/ppermute | solution.py:16
  60.1 8.4 %collective-permute-done.11 = f32[32,24,4]{2,1,0:T(8,128)S(1)} collective-permute-done((f32[32,24,4]{2,1,0:T(8,128)S(1)}, f32[32,24,4]{2,1,0:T(8,128)S(1)}, u32[]{:S(2)}, u32[]{:S(2)}) %collective-permute-start.11) | collective-permute-done | bytes 12320 | tf_op jit(solution)/shard_map/ppermute | solution.py:19
  68.6 0.7 pad_maximum_fusion.5
  69.3 7.7 %collective-permute-done.14 = f32[32,24,4]{2,1,0:T(8,128)S(1)} collective-permute-done((f32[32,24,4]{2,1,0:T(8,128)S(1)}, f32[32,24,4]{2,1,0:T(8,128)S(1)}, u32[]{:S(2)}, u32[]{:S(2)}) %collective-permute-start.14) | collective-permute-done | bytes 12320 | tf_op jit(solution)/shard_map/ppermute | solution.py:16
  77.0 4.4 %collective-permute-done.15 = f32[32,24,4]{2,1,0:T(8,128)S(1)} collective-permute-done((f32[32,24,4]{2,1,0:T(8,128)S(1)}, f32[32,24,4]{2,1,0:T(8,128)S(1)}, u32[]{:S(2)}, u32[]{:S(2)}) %collective-permute-start.15) | collective-permute-done | bytes 12320 | tf_op jit(solution)/shard_map/ppermute | solution.py:19
  81.4 2.1 %fusion.6 = f32[32,22,262]{2,1,0:T(8,128)S(1)} fusion(f32[32,24,4]{2,1,0:T(8,128)S(1)} %collective-permute-done.15, f32[32,24,4]{2,1,0:T(8,128)S(1)} %collective-permute-done.14, f32[32,4,256]{2,1,0:T(4,128)S(1)} %collective-permute-done.13, f32[32,16,256]{2,1,0:T(8,128)S(1)} %get-tuple-element.49, f32[32,4,256]{2,1,0:T(4,128)S(1)} %collective-permute-done.12, ...), kind=kLoop, calls=%fused_computation.15 | loop fusion | flops 2028928 | bytes 5266580 | tf_op jit(solution)/shard_map/sub | solution.py:76
  83.5 1.6 slice_subtract_fusion.1
  85.1 1.6 slice_subtract_fusion
  86.7 1.3 multiply_reduce_fusion.8
  88.1 1.6 %multiply_reduce_fusion.1 = (f32[]{:T(128)}, f32[]{:T(128)}, f32[]{:T(128)}, f32[]{:T(128)}, f32[]{:T(128)}, /*index=5*/f32[]{:T(128)}, f32[]{:T(128)}, f32[]{:T...) fusion(f32[32,16,256]{2,1,0:T(8,128)S(1)} %get-tuple-element.46, ...), kind=kLoop, calls=%fused_computation.63 | loop fusion | flops 4194288 | bytes 4718656 | tf_op jit(solution)/shard_map/reduce_sum | solution.py:82
  89.7 40.1 %all-reduce = (f32[1]{0:T(128)}, f32[1]{0:T(128)}, f32[1]{0:T(128)}, f32[1]{0:T(128)}, f32[1]{0:T(128)}, /*index=5*/f32[1]{0:T(128)}, f32[1]{0:T(128)}, f32[1]{0...) all-reduce(f32[1]{0:T(128)} %bitcast, f32[1]{0:T(128)} %bitcast.1, ...), channel_id=1, replica_groups=mesh['grp'=2,'row'=8,'col'=2] {'grp','row','col'}, use_global_device_ids=true, to_apply=%region_1.2 | all-reduce | flops 17 | bytes 136 | tf_op jit(solution)/shard_map/psum | solution.py:84
  129.8 5.7 %stack.84 = f32[9]{0:T(128)S(1)} concatenate(f32[1]{0:T(128)} %get-tuple-element.27, f32[1]{0:T(128)} %get-tuple-element.28, f32[1]{0:T(128)} %get-tuple-element.29, f32[1]{0:T(128)} %get-tuple-element.30, f32[1]{0:T(128)} %get-tuple-element.31, f32[1]{0:T(128)} %get-tuple-element.32, f32[1]{0:T(128)} %get-tuple-element.33, f32[1]{0:T(128)} %get-tuple-element.34, f32[1]{0:T(128)} %get-tuple-element.35), dimensions={0} | concatenate | bytes 72 | tf_op jit(solution)/shard_map/stack | solution.py:90
  135.5 5.2 %stack.93 = f32[8]{0:T(128)S(1)} concatenate(f32[1]{0:T(128)} %get-tuple-element.36, f32[1]{0:T(128)} %get-tuple-element.37, f32[1]{0:T(128)} %get-tuple-element.38, f32[1]{0:T(128)} %get-tuple-element.39, f32[1]{0:T(128)} %get-tuple-element.40, f32[1]{0:T(128)} %get-tuple-element.41, f32[1]{0:T(128)} %get-tuple-element.42, f32[1]{0:T(128)} %get-tuple-element.43), dimensions={0} | concatenate | bytes 64 | tf_op jit(solution)/shard_map/stack | solution.py:91
  160.2 1.9 %stack.94 = f32[17]{0:T(128)} concatenate(f32[1]{0:T(128)} %get-tuple-element.73, f32[1]{0:T(128)} %get-tuple-element.82, f32[1]{0:T(128)S(6)} %sub.120, f32[1]{0:T(128)S(6)} %sub.121, f32[1]{0:T(128)S(6)} %sub.122, f32[1]{0:T(128)S(6)} %sub.123, f32[1]{0:T(128)S(6)} %sub.124, f32[1]{0:T(128)S(6)} %sub.125, f32[1]{0:T(128)S(6)} %sub.126, f32[1]{0:T(128)S(6)} %sub.127, ...), dimensions={0} | concatenate | bytes 136 | tf_op jit(solution)/shard_map/stack | solution.py:101
  (47 shorter events, 5.4 us)
Async XLA Ops:
  1.4 9.6 %collective-permute-start = (f32[4,256]{1,0:T(4,128)S(1)}, f32[4,256]{1,0:T(4,128)S(1)}, u32[]{:S(2)}, u32[]{:S(2)}) collective-permute-start(f32[4,256]{1,0:T(4,128)S(1)} %get-tuple-element.63), channel_id=1, source_target_pairs={{0,2},{2,4},{4,6},{6,8},{8,10},{10,12},{12,14},{14,0},{1,3},{3,5},... | collective-permute-start | bytes 12296 | tf_op jit(solution)/shard_map/ppermute | solution.py:16
  1.8 9.1 %collective-permute-start.1 = (f32[4,256]{1,0:T(4,128)S(1)}, f32[4,256]{1,0:T(4,128)S(1)}, u32[]{:S(2)}, u32[]{:S(2)}) collective-permute-start(f32[4,256]{1,0:T(4,128)S(1)} %get-tuple-element.64), channel_id=1, source_target_pairs={{2,0},{4,2},{6,4},{8,6},{10,8},{12,10},{14,12},{0,14},{3,1},{5,3},... | collective-permute-start | bytes 12296 | tf_op jit(solution)/shard_map/ppermute | solution.py:19
  7.0 6.9 %collective-permute-start.4 = (f32[32,4,256]{2,1,0:T(4,128)S(1)}, f32[32,4,256]{2,1,0:T(4,128)S(1)}, u32[]{:S(2)}, u32[]{:S(2)}) collective-permute-start(f32[32,4,256]{2,1,0:T(4,128)S(1)} %get-tuple-element.59), channel_id=1, source_target_pairs={{0,2},{2,4},{4,6},{6,8},{8,10},{10,12},{12,14},{14,0},{1,3},{3,5},... | collective-permute-start | bytes 393224 | tf_op jit(solution)/shard_map/ppermute | solution.py:16
  7.0 6.8 %collective-permute-start.5 = (f32[32,4,256]{2,1,0:T(4,128)S(1)}, f32[32,4,256]{2,1,0:T(4,128)S(1)}, u32[]{:S(2)}, u32[]{:S(2)}) collective-permute-start(f32[32,4,256]{2,1,0:T(4,128)S(1)} %get-tuple-element.60), channel_id=1, source_target_pairs={{2,0},{4,2},{6,4},{8,6},{10,8},{12,10},{14,12},{0,14},{3,1},{5,3},... | collective-permute-start | bytes 393224 | tf_op jit(solution)/shard_map/ppermute | solution.py:19
  11.7 6.1 %collective-permute-start.2 = (f32[24,4]{1,0:T(8,128)S(1)}, f32[24,4]{1,0:T(8,128)S(1)}, u32[]{:S(2)}, u32[]{:S(2)}) collective-permute-start(f32[24,4]{1,0:T(8,128)S(1)} %get-tuple-element.61), channel_id=1, source_target_pairs={{0,1},{1,0},{2,3},{3,2},{4,5},{5,4},{6,7},{7,6},{8,9},{9,8},{10,11... | collective-permute-start | bytes 1160 | tf_op jit(solution)/shard_map/ppermute | solution.py:16
  13.7 4.1 %collective-permute-start.3 = (f32[24,4]{1,0:T(8,128)S(1)}, f32[24,4]{1,0:T(8,128)S(1)}, u32[]{:S(2)}, u32[]{:S(2)}) collective-permute-start(f32[24,4]{1,0:T(8,128)S(1)} %get-tuple-element.62), channel_id=1, source_target_pairs={{1,0},{0,1},{3,2},{2,3},{5,4},{4,5},{7,6},{6,7},{9,8},{8,9},{11,10... | collective-permute-start | bytes 1160 | tf_op jit(solution)/shard_map/ppermute | solution.py:19
  15.0 2.8 %copy-start.3 = (f32[16,256]{1,0:T(8,128)S(1)}, f32[16,256]{1,0:T(8,128)}, u32[]{:S(2)}) copy-start(f32[16,256]{1,0:T(8,128)} %param.3) | copy-start | bytes 49156
  15.0 19.1 %copy-start = (f32[32,16,256]{2,1,0:T(8,128)S(1)}, f32[32,16,256]{2,1,0:T(8,128)}, u32[]{:S(2)}) copy-start(f32[32,16,256]{2,1,0:T(8,128)} %param.2) | copy-start | bytes 1572868
  15.2 12.5 %collective-permute-start.6 = (f32[32,24,4]{2,1,0:T(8,128)S(1)}, f32[32,24,4]{2,1,0:T(8,128)S(1)}, u32[]{:S(2)}, u32[]{:S(2)}) collective-permute-start(f32[32,24,4]{2,1,0:T(8,128)S(1)} %get-tuple-element.55), channel_id=1, source_target_pairs={{0,1},{1,0},{2,3},{3,2},{4,5},{5,4},{6,7},{7,6},{8,9},{9,8},{10,11... | collective-permute-start | bytes 36872 | tf_op jit(solution)/shard_map/ppermute | solution.py:16
  17.7 16.3 %collective-permute-start.7 = (f32[32,24,4]{2,1,0:T(8,128)S(1)}, f32[32,24,4]{2,1,0:T(8,128)S(1)}, u32[]{:S(2)}, u32[]{:S(2)}) collective-permute-start(f32[32,24,4]{2,1,0:T(8,128)S(1)} %get-tuple-element.56), channel_id=1, source_target_pairs={{1,0},{0,1},{3,2},{2,3},{5,4},{4,5},{7,6},{6,7},{9,8},{8,9},{11,10... | collective-permute-start | bytes 36872 | tf_op jit(solution)/shard_map/ppermute | solution.py:19
  40.1 7.6 %collective-permute-start.8 = (f32[32,4,256]{2,1,0:T(4,128)S(1)}, f32[32,4,256]{2,1,0:T(4,128)S(1)}, u32[]{:S(2)}, u32[]{:S(2)}) collective-permute-start(f32[32,4,256]{2,1,0:T(4,128)S(1)} %get-tuple-element.57), channel_id=1, source_target_pairs={{0,2},{2,4},{4,6},{6,8},{8,10},{10,12},{12,14},{14,0},{1,3},{3,5},... | collective-permute-start | bytes 393224 | tf_op jit(solution)/shard_map/ppermute | solution.py:16
  40.2 7.6 %collective-permute-start.9 = (f32[32,4,256]{2,1,0:T(4,128)S(1)}, f32[32,4,256]{2,1,0:T(4,128)S(1)}, u32[]{:S(2)}, u32[]{:S(2)}) collective-permute-start(f32[32,4,256]{2,1,0:T(4,128)S(1)} %get-tuple-element.58), channel_id=1, source_target_pairs={{2,0},{4,2},{6,4},{8,6},{10,8},{12,10},{14,12},{0,14},{3,1},{5,3},... | collective-permute-start | bytes 393224 | tf_op jit(solution)/shard_map/ppermute | solution.py:19
  43.9 6.3 %collective-permute-start.12 = (f32[32,4,256]{2,1,0:T(4,128)S(1)}, f32[32,4,256]{2,1,0:T(4,128)S(1)}, u32[]{:S(2)}, u32[]{:S(2)}) collective-permute-start(f32[32,4,256]{2,1,0:T(4,128)S(1)} %get-tuple-element.47), channel_id=1, source_target_pairs={{0,2},{2,4},{4,6},{6,8},{8,10},{10,12},{12,14},{14,0},{1,3},{3,5},... | collective-permute-start | bytes 393224 | tf_op jit(solution)/shard_map/ppermute | solution.py:16
  44.0 6.3 %collective-permute-start.13 = (f32[32,4,256]{2,1,0:T(4,128)S(1)}, f32[32,4,256]{2,1,0:T(4,128)S(1)}, u32[]{:S(2)}, u32[]{:S(2)}) collective-permute-start(f32[32,4,256]{2,1,0:T(4,128)S(1)} %get-tuple-element.48), channel_id=1, source_target_pairs={{2,0},{4,2},{6,4},{8,6},{10,8},{12,10},{14,12},{0,14},{3,1},{5,3},... | collective-permute-start | bytes 393224 | tf_op jit(solution)/shard_map/ppermute | solution.py:19
  48.1 12.1 %collective-permute-start.10 = (f32[32,24,4]{2,1,0:T(8,128)S(1)}, f32[32,24,4]{2,1,0:T(8,128)S(1)}, u32[]{:S(2)}, u32[]{:S(2)}) collective-permute-start(f32[32,24,4]{2,1,0:T(8,128)S(1)} %get-tuple-element.53), channel_id=1, source_target_pairs={{0,1},{1,0},{2,3},{3,2},{4,5},{5,4},{6,7},{7,6},{8,9},{9,8},{10,11... | collective-permute-start | bytes 36872 | tf_op jit(solution)/shard_map/ppermute | solution.py:16
  48.4 20.2 %collective-permute-start.11 = (f32[32,24,4]{2,1,0:T(8,128)S(1)}, f32[32,24,4]{2,1,0:T(8,128)S(1)}, u32[]{:S(2)}, u32[]{:S(2)}) collective-permute-start(f32[32,24,4]{2,1,0:T(8,128)S(1)} %get-tuple-element.54), channel_id=1, source_target_pairs={{1,0},{0,1},{3,2},{2,3},{5,4},{4,5},{7,6},{6,7},{9,8},{8,9},{11,10... | collective-permute-start | bytes 36872 | tf_op jit(solution)/shard_map/ppermute | solution.py:19
  50.6 26.4 %collective-permute-start.14 = (f32[32,24,4]{2,1,0:T(8,128)S(1)}, f32[32,24,4]{2,1,0:T(8,128)S(1)}, u32[]{:S(2)}, u32[]{:S(2)}) collective-permute-start(f32[32,24,4]{2,1,0:T(8,128)S(1)} %get-tuple-element.51), channel_id=1, source_target_pairs={{0,1},{1,0},{2,3},{3,2},{4,5},{5,4},{6,7},{7,6},{8,9},{9,8},{10,11... | collective-permute-start | bytes 36872 | tf_op jit(solution)/shard_map/ppermute | solution.py:16
  51.3 30.1 %collective-permute-start.15 = (f32[32,24,4]{2,1,0:T(8,128)S(1)}, f32[32,24,4]{2,1,0:T(8,128)S(1)}, u32[]{:S(2)}, u32[]{:S(2)}) collective-permute-start(f32[32,24,4]{2,1,0:T(8,128)S(1)} %get-tuple-element.52), channel_id=1, source_target_pairs={{1,0},{0,1},{3,2},{2,3},{5,4},{4,5},{7,6},{6,7},{9,8},{8,9},{11,10... | collective-permute-start | bytes 36872 | tf_op jit(solution)/shard_map/ppermute | solution.py:19
  88.1 1.7 %copy-start.1 = (f32[32,16,256]{2,1,0:T(8,128)}, f32[32,16,256]{2,1,0:T(8,128)S(1)}, u32[]{:S(2)}) copy-start(f32[32,16,256]{2,1,0:T(8,128)S(1)} %get-tuple-element.45) | copy-start | bytes 1572868
  88.1 1.7 %copy-start.2 = (f32[32,16,256]{2,1,0:T(8,128)}, f32[32,16,256]{2,1,0:T(8,128)S(1)}, u32[]{:S(2)}) copy-start(f32[32,16,256]{2,1,0:T(8,128)S(1)} %get-tuple-element.46) | copy-start | bytes 1572868
where the time goes:
time: 163 us; the launch traced here: 162 us
  waiting for transfers between devices  44.3 us (27%)
  blocking collectives  40.1 us (25%)
  starting transfers between devices  24.2 us (15%)
  between operations  19.6 us (12%)
  other arithmetic  17.3 us (11%)
  local copies, waits for them, and re-layouts  16.7 us (10%)
    psum x1, blocking collectives, body(): total_squares = [lax.psum(squares[0], ('grp', 'row', 'col'))]  40.1 us
    ppermute x8, waiting for transfers between devices, extended(): lax.ppermute(lax.slice_in_dim(block, block.shape[dim] - width, None, axis...  25.1 us
    ppermute x8, waiting for transfers between devices, extended(): lax.ppermute(lax.slice_in_dim(block, 0, width, axis=dim), axis, backward)  19.2 us
    ppermute x8, starting transfers between devices, extended(): lax.ppermute(lax.slice_in_dim(block, 0, width, axis=dim), axis, backward)  17.9 us
    sub x5, other arithmetic, body(): latest = 2.0 * advance(padded_new) - padded_old[:, 1:-1, 1:-1]  8.54 us
    ppermute x8, starting transfers between devices, extended(): lax.ppermute(lax.slice_in_dim(block, block.shape[dim] - width, None, axis...  6.28 us
    another operation x1, local copies, waits for them, and re-layouts, body(): total_squares = jnp.stack(total_squares)  5.71 us
    another operation x1, local copies, waits for them, and re-layouts, body(): total_crosses = jnp.stack(total_crosses)  5.19 us
  transfers between devices with their start and end apart: 16, of which 8 were waited for; matrix products, arithmetic and copies ran while one was open for 3% of the time, Pallas kernels for 0%

commit v1 on v0

--- a/solution.py
+++ b/solution.py
@@ -81,7 +81,7 @@
             squares.append(jnp.sum(kept_new * kept_new))
             crosses.append(jnp.sum(kept_new * kept_old))
         older, newer = (padded_old, padded_new)
-    total_squares = [lax.psum(squares[0], ("grp", "row", "col"))]
+    total_squares = [lax.psum(lax.psum(squares[0], ("row", "col")), "grp")]
     total_crosses = []
     for index in range(STEPS):
         pair = lax.psum((squares[index + 1], crosses[index]), ("grp", "row", "col"))

time: 163 us -> 200 us (1.23)
  blocking collectives: 40.1 us -> 75.8 us
    psum x1 -> x3, blocking collectives: 40.1 us -> 75.8 us  [the longest x2 38.4 us: body(): total_squares = [lax.psum(lax.psum(squares[0], ('row', 'col')), 'grp')]]
where the time goes in v1:
time: 200 us; the launch traced here: 198 us
  blocking collectives  75.8 us (38%)
  waiting for transfers between devices  44.3 us (22%)
  starting transfers between devices  24.2 us (12%)
  between operations  19.6 us (10%)
  other arithmetic  17.3 us (9%)
  local copies, waits for them, and re-layouts  16.7 us (8%)
    psum x2, blocking collectives, body(): total_squares = [lax.psum(lax.psum(squares[0], ('row', 'col')), 'grp')]  38.4 us
    psum x1, blocking collectives, body(): pair = lax.psum((squares[index + 1], crosses[index]), ('grp', 'row', 'col'))  37.4 us
    ppermute x8, waiting for transfers between devices, extended(): lax.ppermute(lax.slice_in_dim(block, block.shape[dim] - width, None, axis...  25.1 us
    ppermute x8, waiting for transfers between devices, extended(): lax.ppermute(lax.slice_in_dim(block, 0, width, axis=dim), axis, backward)  19.2 us
    ppermute x8, starting transfers between devices, extended(): lax.ppermute(lax.slice_in_dim(block, 0, width, axis=dim), axis, backward)  17.9 us
    sub x5, other arithmetic, body(): latest = 2.0 * advance(padded_new) - padded_old[:, 1:-1, 1:-1]  8.54 us
    ppermute x8, starting transfers between devices, extended(): lax.ppermute(lax.slice_in_dim(block, block.shape[dim] - width, None, axis...  6.28 us
    another operation x1, local copies, waits for them, and re-layouts, body(): total_squares = jnp.stack(total_squares)  5.71 us
  transfers between devices with their start and end apart: 16, of which 8 were waited for; matrix products, arithmetic and copies ran while one was open for 3% of the time, Pallas kernels for 0%

profile of v1, /device:TPU:0, one launch (start us, length us, event | category | flops | bytes accessed | tf_op | source)
XLA Modules:
  0.0 197.8 jit_solution(1050548068692872570)
XLA Ops:
  1.8 4.0 %collective-permute-start.1 = (f32[4,256]{1,0:T(4,128)S(1)}, f32[4,256]{1,0:T(4,128)S(1)}, u32[]{:S(2)}, u32[]{:S(2)}) collective-permute-start(f32[4,256]{1,0:T(4,128)S(1)} %get-tuple-element.63), channel_id=1, source_target_pairs={{2,0},{4,2},{6,4},{8,6},{10,8},{12,10},{14,12},{0,14},{3,1},{5,3},... | collective-permute-start | bytes 12296 | tf_op jit(solution)/shard_map/ppermute | solution.py:19
  5.9 1.1 fusion.39
  7.0 3.5 %collective-permute-start.5 = (f32[32,4,256]{2,1,0:T(4,128)S(1)}, f32[32,4,256]{2,1,0:T(4,128)S(1)}, u32[]{:S(2)}, u32[]{:S(2)}) collective-permute-start(f32[32,4,256]{2,1,0:T(4,128)S(1)} %get-tuple-element.59), channel_id=1, source_target_pairs={{2,0},{4,2},{6,4},{8,6},{10,8},{12,10},{14,12},{0,14},{3,1},{5,3},... | collective-permute-start | bytes 393224 | tf_op jit(solution)/shard_map/ppermute | solution.py:19
  11.7 2.0 %collective-permute-start.2 = (f32[24,4]{1,0:T(8,128)S(1)}, f32[24,4]{1,0:T(8,128)S(1)}, u32[]{:S(2)}, u32[]{:S(2)}) collective-permute-start(f32[24,4]{1,0:T(8,128)S(1)} %get-tuple-element.60), channel_id=1, source_target_pairs={{0,1},{1,0},{2,3},{3,2},{4,5},{5,4},{6,7},{7,6},{8,9},{9,8},{10,11... | collective-permute-start | bytes 1160 | tf_op jit(solution)/shard_map/ppermute | solution.py:16
  13.8 1.2 pad_maximum_fusion.6
  15.2 2.6 %collective-permute-start.6 = (f32[32,24,4]{2,1,0:T(8,128)S(1)}, f32[32,24,4]{2,1,0:T(8,128)S(1)}, u32[]{:S(2)}, u32[]{:S(2)}) collective-permute-start(f32[32,24,4]{2,1,0:T(8,128)S(1)} %get-tuple-element.54), channel_id=1, source_target_pairs={{0,1},{1,0},{2,3},{3,2},{4,5},{5,4},{6,7},{7,6},{8,9},{9,8},{10,11... | collective-permute-start | bytes 36872 | tf_op jit(solution)/shard_map/ppermute | solution.py:16
  18.2 9.5 %collective-permute-done.6 = f32[32,24,4]{2,1,0:T(8,128)S(1)} collective-permute-done((f32[32,24,4]{2,1,0:T(8,128)S(1)}, f32[32,24,4]{2,1,0:T(8,128)S(1)}, u32[]{:S(2)}, u32[]{:S(2)}) %collective-permute-start.6) | collective-permute-done | bytes 12320 | tf_op jit(solution)/shard_map/ppermute | solution.py:16
  27.7 6.4 %collective-permute-done.7 = f32[32,24,4]{2,1,0:T(8,128)S(1)} collective-permute-done((f32[32,24,4]{2,1,0:T(8,128)S(1)}, f32[32,24,4]{2,1,0:T(8,128)S(1)}, u32[]{:S(2)}, u32[]{:S(2)}) %collective-permute-start.7) | collective-permute-done | bytes 12320 | tf_op jit(solution)/shard_map/ppermute | solution.py:19
  34.8 1.3 fusion.18
  36.1 1.6 slice_subtract_fusion.3
  37.7 1.6 slice_subtract_fusion.2
  39.3 0.7 fusion.34
  40.2 3.5 %collective-permute-start.9 = (f32[32,4,256]{2,1,0:T(4,128)S(1)}, f32[32,4,256]{2,1,0:T(4,128)S(1)}, u32[]{:S(2)}, u32[]{:S(2)}) collective-permute-start(f32[32,4,256]{2,1,0:T(4,128)S(1)} %get-tuple-element.57), channel_id=1, source_target_pairs={{2,0},{4,2},{6,4},{8,6},{10,8},{12,10},{14,12},{0,14},{3,1},{5,3},... | collective-permute-start | bytes 393224 | tf_op jit(solution)/shard_map/ppermute | solution.py:19
  44.0 3.5 %collective-permute-start.13 = (f32[32,4,256]{2,1,0:T(4,128)S(1)}, f32[32,4,256]{2,1,0:T(4,128)S(1)}, u32[]{:S(2)}, u32[]{:S(2)}) collective-permute-start(f32[32,4,256]{2,1,0:T(4,128)S(1)} %get-tuple-element.47), channel_id=1, source_target_pairs={{2,0},{4,2},{6,4},{8,6},{10,8},{12,10},{14,12},{0,14},{3,1},{5,3},... | collective-permute-start | bytes 393224 | tf_op jit(solution)/shard_map/ppermute | solution.py:19
  48.4 1.8 collective-permute-start.11
  50.6 0.8 collective-permute-start.14
  51.3 1.3 collective-permute-start.15
  52.7 7.5 %collective-permute-done.10 = f32[32,24,4]{2,1,0:T(8,128)S(1)} collective-permute-done((f32[32,24,4]{2,1,0:T(8,128)S(1)}, f32[32,24,4]{2,1,0:T(8,128)S(1)}, u32[]{:S(2)}, u32[]{:S(2)}) %collective-permute-start.10) | collective-permute-done | bytes 12320 | tf_op jit(solution)/shard_map/ppermute | solution.py:16
  60.1 8.4 %collective-permute-done.11 = f32[32,24,4]{2,1,0:T(8,128)S(1)} collective-permute-done((f32[32,24,4]{2,1,0:T(8,128)S(1)}, f32[32,24,4]{2,1,0:T(8,128)S(1)}, u32[]{:S(2)}, u32[]{:S(2)}) %collective-permute-start.11) | collective-permute-done | bytes 12320 | tf_op jit(solution)/shard_map/ppermute | solution.py:19
  69.3 7.7 %collective-permute-done.14 = f32[32,24,4]{2,1,0:T(8,128)S(1)} collective-permute-done((f32[32,24,4]{2,1,0:T(8,128)S(1)}, f32[32,24,4]{2,1,0:T(8,128)S(1)}, u32[]{:S(2)}, u32[]{:S(2)}) %collective-permute-start.14) | collective-permute-done | bytes 12320 | tf_op jit(solution)/shard_map/ppermute | solution.py:16
  77.0 4.4 %collective-permute-done.15 = f32[32,24,4]{2,1,0:T(8,128)S(1)} collective-permute-done((f32[32,24,4]{2,1,0:T(8,128)S(1)}, f32[32,24,4]{2,1,0:T(8,128)S(1)}, u32[]{:S(2)}, u32[]{:S(2)}) %collective-permute-start.15) | collective-permute-done | bytes 12320 | tf_op jit(solution)/shard_map/ppermute | solution.py:19
  81.4 2.1 %fusion.6 = f32[32,22,262]{2,1,0:T(8,128)S(1)} fusion(f32[32,24,4]{2,1,0:T(8,128)S(1)} %collective-permute-done.15, f32[32,24,4]{2,1,0:T(8,128)S(1)} %collective-permute-done.14, f32[32,4,256]{2,1,0:T(4,128)S(1)} %collective-permute-done.13, f32[32,16,256]{2,1,0:T(8,128)S(1)} %get-tuple-element.48, f32[32,4,256]{2,1,0:T(4,128)S(1)} %collective-permute-done.12, ...), kind=kLoop, calls=%fused_computation.15 | loop fusion | flops 2028928 | bytes 5266580 | tf_op jit(solution)/shard_map/sub | solution.py:76
  83.5 1.6 slice_subtract_fusion.1
  85.1 1.6 slice_subtract_fusion
  86.7 1.3 multiply_reduce_fusion.8
  88.1 1.7 multiply_reduce_fusion.1
  89.7 32.8 %psum.126 = f32[]{:T(128)} all-reduce(f32[]{:T(128)} %get-tuple-element.16), channel_id=1, replica_groups=mesh['grp'=2,'row'=8,'col'=2] {'row','col'}, use_global_device_ids=true, to_apply=%region_1.2 | all-reduce | flops 1 | bytes 8 | tf_op jit(solution)/shard_map/psum | solution.py:84
  122.6 5.6 %psum.127 = f32[1]{0:T(128)} all-reduce(f32[1]{0:T(128)} %bitcast), channel_id=1, replica_groups=mesh['grp'=2,'row'=8,'col'=2] {'grp'}, use_global_device_ids=true, to_apply=%region_2.3 | all-reduce | flops 1 | bytes 8 | tf_op jit(solution)/shard_map/psum | solution.py:84
  128.1 37.4 %all-reduce = (f32[1]{0:T(128)}, f32[1]{0:T(128)}, f32[1]{0:T(128)}, f32[1]{0:T(128)}, f32[1]{0:T(128)}, /*index=5*/f32[1]{0:T(128)}, f32[1]{0:T(128)}, f32[1]{0...) all-reduce(f32[1]{0:T(128)} %bitcast.1, ...), channel_id=1, replica_groups=mesh['grp'=2,'row'=8,'col'=2] {'grp','row','col'}, use_global_device_ids=true, to_apply=%region_4.5 | all-reduce | flops 16 | bytes 128 | tf_op jit(solution)/shard_map/psum | solution.py:87
  165.6 5.7 %stack.84 = f32[9]{0:T(128)S(1)} concatenate(f32[1]{0:T(128)} %psum.127, f32[1]{0:T(128)} %get-tuple-element.27, f32[1]{0:T(128)} %get-tuple-element.28, f32[1]{0:T(128)} %get-tuple-element.29, f32[1]{0:T(128)} %get-tuple-element.30, f32[1]{0:T(128)} %get-tuple-element.31, f32[1]{0:T(128)} %get-tuple-element.32, f32[1]{0:T(128)} %get-tuple-element.33, f32[1]{0:T(128)} %get-tuple-element.34), dimensions={0} | concatenate | bytes 72 | tf_op jit(solution)/shard_map/stack | solution.py:90
  171.3 5.2 %stack.93 = f32[8]{0:T(128)S(1)} concatenate(f32[1]{0:T(128)} %get-tuple-element.35, f32[1]{0:T(128)} %get-tuple-element.36, f32[1]{0:T(128)} %get-tuple-element.37, f32[1]{0:T(128)} %get-tuple-element.38, f32[1]{0:T(128)} %get-tuple-element.39, f32[1]{0:T(128)} %get-tuple-element.40, f32[1]{0:T(128)} %get-tuple-element.41, f32[1]{0:T(128)} %get-tuple-element.42), dimensions={0} | concatenate | bytes 64 | tf_op jit(solution)/shard_map/stack | solution.py:91
  196.0 1.9 stack.94
  (49 shorter events, 6.9 us)
Async XLA Ops:
  1.4 9.6 %collective-permute-start = (f32[4,256]{1,0:T(4,128)S(1)}, f32[4,256]{1,0:T(4,128)S(1)}, u32[]{:S(2)}, u32[]{:S(2)}) collective-permute-start(f32[4,256]{1,0:T(4,128)S(1)} %get-tuple-element.62), channel_id=1, source_target_pairs={{0,2},{2,4},{4,6},{6,8},{8,10},{10,12},{12,14},{14,0},{1,3},{3,5},... | collective-permute-start | bytes 12296 | tf_op jit(solution)/shard_map/ppermute | solution.py:16
  1.8 9.1 %collective-permute-start.1 = (f32[4,256]{1,0:T(4,128)S(1)}, f32[4,256]{1,0:T(4,128)S(1)}, u32[]{:S(2)}, u32[]{:S(2)}) collective-permute-start(f32[4,256]{1,0:T(4,128)S(1)} %get-tuple-element.63), channel_id=1, source_target_pairs={{2,0},{4,2},{6,4},{8,6},{10,8},{12,10},{14,12},{0,14},{3,1},{5,3},... | collective-permute-start | bytes 12296 | tf_op jit(solution)/shard_map/ppermute | solution.py:19
  7.0 6.9 %collective-permute-start.4 = (f32[32,4,256]{2,1,0:T(4,128)S(1)}, f32[32,4,256]{2,1,0:T(4,128)S(1)}, u32[]{:S(2)}, u32[]{:S(2)}) collective-permute-start(f32[32,4,256]{2,1,0:T(4,128)S(1)} %get-tuple-element.58), channel_id=1, source_target_pairs={{0,2},{2,4},{4,6},{6,8},{8,10},{10,12},{12,14},{14,0},{1,3},{3,5},... | collective-permute-start | bytes 393224 | tf_op jit(solution)/shard_map/ppermute | solution.py:16
  7.0 6.8 %collective-permute-start.5 = (f32[32,4,256]{2,1,0:T(4,128)S(1)}, f32[32,4,256]{2,1,0:T(4,128)S(1)}, u32[]{:S(2)}, u32[]{:S(2)}) collective-permute-start(f32[32,4,256]{2,1,0:T(4,128)S(1)} %get-tuple-element.59), channel_id=1, source_target_pairs={{2,0},{4,2},{6,4},{8,6},{10,8},{12,10},{14,12},{0,14},{3,1},{5,3},... | collective-permute-start | bytes 393224 | tf_op jit(solution)/shard_map/ppermute | solution.py:19
  11.7 6.1 %collective-permute-start.2 = (f32[24,4]{1,0:T(8,128)S(1)}, f32[24,4]{1,0:T(8,128)S(1)}, u32[]{:S(2)}, u32[]{:S(2)}) collective-permute-start(f32[24,4]{1,0:T(8,128)S(1)} %get-tuple-element.60), channel_id=1, source_target_pairs={{0,1},{1,0},{2,3},{3,2},{4,5},{5,4},{6,7},{7,6},{8,9},{9,8},{10,11... | collective-permute-start | bytes 1160 | tf_op jit(solution)/shard_map/ppermute | solution.py:16
  13.7 4.1 %collective-permute-start.3 = (f32[24,4]{1,0:T(8,128)S(1)}, f32[24,4]{1,0:T(8,128)S(1)}, u32[]{:S(2)}, u32[]{:S(2)}) collective-permute-start(f32[24,4]{1,0:T(8,128)S(1)} %get-tuple-element.61), channel_id=1, source_target_pairs={{1,0},{0,1},{3,2},{2,3},{5,4},{4,5},{7,6},{6,7},{9,8},{8,9},{11,10... | collective-permute-start | bytes 1160 | tf_op jit(solution)/shard_map/ppermute | solution.py:19
  15.0 2.8 %copy-start.3 = (f32[16,256]{1,0:T(8,128)S(1)}, f32[16,256]{1,0:T(8,128)}, u32[]{:S(2)}) copy-start(f32[16,256]{1,0:T(8,128)} %param.3) | copy-start | bytes 49156
  15.0 19.1 %copy-start = (f32[32,16,256]{2,1,0:T(8,128)S(1)}, f32[32,16,256]{2,1,0:T(8,128)}, u32[]{:S(2)}) copy-start(f32[32,16,256]{2,1,0:T(8,128)} %param.2) | copy-start | bytes 1572868
  15.2 12.5 %collective-permute-start.6 = (f32[32,24,4]{2,1,0:T(8,128)S(1)}, f32[32,24,4]{2,1,0:T(8,128)S(1)}, u32[]{:S(2)}, u32[]{:S(2)}) collective-permute-start(f32[32,24,4]{2,1,0:T(8,128)S(1)} %get-tuple-element.54), channel_id=1, source_target_pairs={{0,1},{1,0},{2,3},{3,2},{4,5},{5,4},{6,7},{7,6},{8,9},{9,8},{10,11... | collective-permute-start | bytes 36872 | tf_op jit(solution)/shard_map/ppermute | solution.py:16
  17.7 16.3 %collective-permute-start.7 = (f32[32,24,4]{2,1,0:T(8,128)S(1)}, f32[32,24,4]{2,1,0:T(8,128)S(1)}, u32[]{:S(2)}, u32[]{:S(2)}) collective-permute-start(f32[32,24,4]{2,1,0:T(8,128)S(1)} %get-tuple-element.55), channel_id=1, source_target_pairs={{1,0},{0,1},{3,2},{2,3},{5,4},{4,5},{7,6},{6,7},{9,8},{8,9},{11,10... | collective-permute-start | bytes 36872 | tf_op jit(solution)/shard_map/ppermute | solution.py:19
  40.1 7.6 %collective-permute-start.8 = (f32[32,4,256]{2,1,0:T(4,128)S(1)}, f32[32,4,256]{2,1,0:T(4,128)S(1)}, u32[]{:S(2)}, u32[]{:S(2)}) collective-permute-start(f32[32,4,256]{2,1,0:T(4,128)S(1)} %get-tuple-element.56), channel_id=1, source_target_pairs={{0,2},{2,4},{4,6},{6,8},{8,10},{10,12},{12,14},{14,0},{1,3},{3,5},... | collective-permute-start | bytes 393224 | tf_op jit(solution)/shard_map/ppermute | solution.py:16
  40.2 7.6 %collective-permute-start.9 = (f32[32,4,256]{2,1,0:T(4,128)S(1)}, f32[32,4,256]{2,1,0:T(4,128)S(1)}, u32[]{:S(2)}, u32[]{:S(2)}) collective-permute-start(f32[32,4,256]{2,1,0:T(4,128)S(1)} %get-tuple-element.57), channel_id=1, source_target_pairs={{2,0},{4,2},{6,4},{8,6},{10,8},{12,10},{14,12},{0,14},{3,1},{5,3},... | collective-permute-start | bytes 393224 | tf_op jit(solution)/shard_map/ppermute | solution.py:19
  43.9 6.3 %collective-permute-start.12 = (f32[32,4,256]{2,1,0:T(4,128)S(1)}, f32[32,4,256]{2,1,0:T(4,128)S(1)}, u32[]{:S(2)}, u32[]{:S(2)}) collective-permute-start(f32[32,4,256]{2,1,0:T(4,128)S(1)} %get-tuple-element.46), channel_id=1, source_target_pairs={{0,2},{2,4},{4,6},{6,8},{8,10},{10,12},{12,14},{14,0},{1,3},{3,5},... | collective-permute-start | bytes 393224 | tf_op jit(solution)/shard_map/ppermute | solution.py:16
  44.0 6.3 %collective-permute-start.13 = (f32[32,4,256]{2,1,0:T(4,128)S(1)}, f32[32,4,256]{2,1,0:T(4,128)S(1)}, u32[]{:S(2)}, u32[]{:S(2)}) collective-permute-start(f32[32,4,256]{2,1,0:T(4,128)S(1)} %get-tuple-element.47), channel_id=1, source_target_pairs={{2,0},{4,2},{6,4},{8,6},{10,8},{12,10},{14,12},{0,14},{3,1},{5,3},... | collective-permute-start | bytes 393224 | tf_op jit(solution)/shard_map/ppermute | solution.py:19
  48.1 12.1 %collective-permute-start.10 = (f32[32,24,4]{2,1,0:T(8,128)S(1)}, f32[32,24,4]{2,1,0:T(8,128)S(1)}, u32[]{:S(2)}, u32[]{:S(2)}) collective-permute-start(f32[32,24,4]{2,1,0:T(8,128)S(1)} %get-tuple-element.52), channel_id=1, source_target_pairs={{0,1},{1,0},{2,3},{3,2},{4,5},{5,4},{6,7},{7,6},{8,9},{9,8},{10,11... | collective-permute-start | bytes 36872 | tf_op jit(solution)/shard_map/ppermute | solution.py:16
  48.4 20.2 %collective-permute-start.11 = (f32[32,24,4]{2,1,0:T(8,128)S(1)}, f32[32,24,4]{2,1,0:T(8,128)S(1)}, u32[]{:S(2)}, u32[]{:S(2)}) collective-permute-start(f32[32,24,4]{2,1,0:T(8,128)S(1)} %get-tuple-element.53), channel_id=1, source_target_pairs={{1,0},{0,1},{3,2},{2,3},{5,4},{4,5},{7,6},{6,7},{9,8},{8,9},{11,10... | collective-permute-start | bytes 36872 | tf_op jit(solution)/shard_map/ppermute | solution.py:19
  50.6 26.4 %collective-permute-start.14 = (f32[32,24,4]{2,1,0:T(8,128)S(1)}, f32[32,24,4]{2,1,0:T(8,128)S(1)}, u32[]{:S(2)}, u32[]{:S(2)}) collective-permute-start(f32[32,24,4]{2,1,0:T(8,128)S(1)} %get-tuple-element.50), channel_id=1, source_target_pairs={{0,1},{1,0},{2,3},{3,2},{4,5},{5,4},{6,7},{7,6},{8,9},{9,8},{10,11... | collective-permute-start | bytes 36872 | tf_op jit(solution)/shard_map/ppermute | solution.py:16
  51.3 30.1 %collective-permute-start.15 = (f32[32,24,4]{2,1,0:T(8,128)S(1)}, f32[32,24,4]{2,1,0:T(8,128)S(1)}, u32[]{:S(2)}, u32[]{:S(2)}) collective-permute-start(f32[32,24,4]{2,1,0:T(8,128)S(1)} %get-tuple-element.51), channel_id=1, source_target_pairs={{1,0},{0,1},{3,2},{2,3},{5,4},{4,5},{7,6},{6,7},{9,8},{8,9},{11,10... | collective-permute-start | bytes 36872 | tf_op jit(solution)/shard_map/ppermute | solution.py:19
  88.1 1.7 copy-start.1
  88.1 1.7 copy-start.2
